TPU v7x, 32 devices: a whole 2x2x4 slice. The times are simulated.
32 devices in a mesh: blk: 4 (over x, core), vox: 8 (over z, y).
Axes of the slice: x: 2, y: 2, z: 4, core: 2. Of those that a mesh axis runs over, the one named last changes fastest.
Arguments:
- src_fields: bfloat16 [256, 32768], P('blk', 'vox'), may hold values from -6 to 6
- det_fields: bfloat16 [256, 32768], P('blk', 'vox'), may hold values from -6 to 6
- probes: bfloat16 [2, 32768], P(None, 'vox'), may hold values from -6 to 6
Outputs:
- curvature: float32 [2, 32768], P(None, 'vox')
All inputs are finite; a program needn't handle non-finite values.
Results may differ from a plain program's by a relative error of at most 0.0016.
Values may be sent and summed in bfloat16 or wider, within the bound.
No kernel may reach another device: no remote copies, remote signals or barrier semaphores. Data moves between devices by JAX's collectives and lax.ppermute only.
A program may use at most 64 MiB of HBM per device.

v0:
```python
import jax
import jax.numpy as jnp
from jax import lax
from jax.sharding import PartitionSpec as P


def shards(src_fields, det_fields, probes):
    src_count, vox_count = src_fields.shape
    det_count = det_fields.shape[0]
    groups = lax.axis_size("blk")
    det_total = det_count * groups
    probe_count = probes.shape[0]
    weighted = (src_fields.astype(jnp.float32)[None] * probes.astype(jnp.float32)[:, None]).astype(
        jnp.bfloat16
    )
    weighted = weighted.reshape(probe_count * src_count, vox_count)
    slab = jnp.zeros((0, vox_count), jnp.bfloat16)
    product = jnp.einsum(
        "rv,dv->rd",
        weighted,
        lax.all_gather(det_fields, "blk", axis=0, tiled=True),
        preferred_element_type=jnp.float32,
    )
    partial_value, slab = (product, slab)
    measured = lax.psum(partial_value, "vox")
    measured_b = measured.astype(jnp.bfloat16)
    backproj = jnp.dot(
        measured_b,
        lax.all_gather(det_fields, "blk", axis=0, tiled=True),
        preferred_element_type=jnp.float32,
    )
    backproj = backproj.reshape(probe_count, src_count, vox_count)
    contrib = jnp.sum(src_fields.astype(jnp.float32)[None] * backproj, axis=1)
    total = lax.psum(contrib, "blk")
    normalizer = jnp.float32(1.0 / (src_count * groups * det_total))
    return total * normalizer


def solution(mesh):
    return jax.shard_map(
        shards,
        mesh=mesh,
        in_specs=(P("blk", "vox"), P("blk", "vox"), P(None, "vox")),
        out_specs=P(None, "vox"),
        check_vma=False,
    )
```

profile of v0, /device:TPU:0, one launch (start us, length us, event | category | flops | bytes accessed | tf_op | source)
XLA Modules:
  0.0 93.9 jit_solution(10206651195195280861)
XLA Ops:
  6.5 0.0 all-gather.2.cloned.1.call-start
  6.5 0.7 all-gather.2.cloned.1.call-update
  7.3 0.7 convert_element_type.18
  8.0 1.1 %convert_element_type.17 = f32[64,4096]{1,0:T(8,128)S(1)} convert(bf16[64,4096]{1,0:T(8,128)(2,1)} %param.3) | non-fusion elementwise | flops 262144 | bytes 1572864 | tf_op jit(solution)/shard_map/convert_element_type | solution.py:33
  9.1 1.1 %multiply_convert_fusion = bf16[2,64,4096]{2,1,0:T(8,128)(2,1)} fusion(f32[2,4096]{1,0:T(2,128)S(1)} %convert_element_type.18, f32[64,4096]{1,0:T(8,128)S(1)} %convert_element_type.17), kind=kLoop, calls=%fused_computation.1 | loop fusion | flops 1048576 | bytes 2129920 | tf_op jit(solution)/shard_map/convert_element_type | solution.py:13
  10.3 24.0 %all-gather.2.cloned.1.call-done = bf16[256,4096]{1,0:T(8,128)(2,1)} async-done(((bf16[64,4096]{1,0:T(8,128)(2,1)}), bf16[256,4096]{1,0:T(8,128)(2,1)}) %all-gather.2.cloned.1.call-update) | async-done | bytes 2097168 | tf_op jit(solution)/shard_map/all_gather | solution.py:21
  34.2 0.0 copy-start
  34.2 2.9 %fusion.2 = f32[128,256]{1,0:T(8,128)S(1)} fusion(bf16[128,4096]{1,0:T(8,128)(2,1)} %bitcast.7, bf16[256,4096]{1,0:T(8,128)(2,1)} %all-gather.2.cloned.1.call-done), kind=kOutput, calls=%fused_computation.5 | convolution fusion | flops 268435456 | bytes 3276800 | tf_op jit(solution)/shard_map/rv,dv->rd/dot_general | solution.py:18
  37.1 38.3 %all-reduce.1 = bf16[128,256]{1,0:T(8,128)(2,1)S(1)} all-reduce(f32[128,256]{1,0:T(8,128)S(1)} %fusion.2), channel_id=1, replica_groups=mesh['blk'=4,'vox'=8] {'vox'}, use_global_device_ids=true, to_apply=%region_0.0 | all-reduce | flops 32768 | bytes 196608 | tf_op jit(solution)/shard_map/psum | solution.py:25
  75.5 0.0 copy-done
  75.5 0.5 multiply_reduce_fusion
  76.0 10.4 %psum.15 = f32[2,4096]{1,0:T(2,128)S(1)} all-reduce(f32[2,4096]{1,0:T(2,128)S(1)} %multiply_reduce_fusion), channel_id=1, replica_groups=mesh['blk'=4,'vox'=8] {'blk'}, use_global_device_ids=true, to_apply=%region_2.0 | all-reduce | flops 8192 | bytes 65536 | tf_op jit(solution)/shard_map/psum | solution.py:34
  86.4 0.6 broadcast_multiply_fusion
Async XLA Ops:
  6.5 27.7 %all-gather.2.cloned.1.call-start = ((), (), s32[]{:S(2)}) async-start(), calls=%async_computation | async-start | bytes 2621440 | tf_op jit(solution)/shard_map/all_gather | solution.py:21
  34.2 41.2 %copy-start = (bf16[256,4096]{1,0:T(8,128)(2,1)S(1)}, bf16[256,4096]{1,0:T(8,128)(2,1)}, u32[]{:S(2)}) copy-start(bf16[256,4096]{1,0:T(8,128)(2,1)} %all-gather.2.cloned.1.call-done) | copy-start | bytes 6291460
Sparse Core Ops, SparseCore 0:
  8.9 25.2 all-gather.1
where the time goes:
time: 94.1 us; the launch traced here: 93.9 us
  blocking collectives  48.8 us (52%)
  waiting for transfers between devices  24.7 us (26%)
  between operations  13.4 us (14%)
  other arithmetic  3.62 us (4%)
  matrix products  3.39 us (4%)
    psum x1, blocking collectives, shards(): measured = lax.psum(partial_value, 'vox')  38.3 us
    all_gather x1, waiting for transfers between devices, shards(): lax.all_gather(det_fields, 'blk', axis=0, tiled=True)  24 us
    psum x1, blocking collectives, shards(): total = lax.psum(contrib, 'blk')  10.4 us
    dot_general x1, matrix products, shards(): jnp.einsum('rv,dv->rd', weighted, lax.all_gather(det_fields, 'blk', axis=...  2.89 us
  transfers between devices with their start and end apart: 1, of which 1 were waited for; matrix products, arithmetic and copies ran while one was open for 3% of the time, Pallas kernels for 0%

commit v1 on v0

--- a/solution.py
+++ b/solution.py
@@ -31,7 +31,8 @@
     )
     backproj = backproj.reshape(probe_count, src_count, vox_count)
     contrib = jnp.sum(src_fields.astype(jnp.float32)[None] * backproj, axis=1)
-    total = lax.psum(contrib, "blk")
+    shards_2 = lax.all_gather(contrib, "blk", axis=0, tiled=False)
+    total = shards_2.sum(axis=0)
     normalizer = jnp.float32(1.0 / (src_count * groups * det_total))
     return total * normalizer
 

time: 94.1 us -> 89.2 us (0.948)
  blocking collectives: 48.8 us -> 43.8 us
    psum x1 -> x0, blocking collectives: 10.4 us -> none  [shards(): total = lax.psum(contrib, 'blk')]
    all_gather x0 -> x1, blocking collectives: none -> 5.42 us  [shards(): shards_2 = lax.all_gather(contrib, 'blk', axis=0, tiled=False)]
where the time goes in v1:
time: 89.2 us; the launch traced here: 88.9 us
  blocking collectives  43.8 us (49%)
  waiting for transfers between devices  24.7 us (28%)
  between operations  13.4 us (15%)
  other arithmetic  3.67 us (4%)
  matrix products  3.39 us (4%)
    psum x1, blocking collectives, shards(): measured = lax.psum(partial_value, 'vox')  38.3 us
    all_gather x1, waiting for transfers between devices, shards(): lax.all_gather(det_fields, 'blk', axis=0, tiled=True)  24 us
    all_gather x1, blocking collectives, shards(): shards_2 = lax.all_gather(contrib, 'blk', axis=0, tiled=False)  5.42 us
    dot_general x1, matrix products, shards(): jnp.einsum('rv,dv->rd', weighted, lax.all_gather(det_fields, 'blk', axis=...  2.89 us
  transfers between devices with their start and end apart: 1, of which 1 were waited for; matrix products, arithmetic and copies ran while one was open for 3% of the time, Pallas kernels for 0%

profile of v1, /device:TPU:0, one launch (start us, length us, event | category | flops | bytes accessed | tf_op | source)
XLA Modules:
  0.0 88.9 jit_solution(7705705265304068397)
XLA Ops:
  6.5 0.0 all-gather.4.cloned.1.call-start
  6.5 0.7 all-gather.4.cloned.1.call-update
  7.3 0.7 convert_element_type.18
  8.0 1.1 %convert_element_type.17 = f32[64,4096]{1,0:T(8,128)S(1)} convert(bf16[64,4096]{1,0:T(8,128)(2,1)} %param.3) | non-fusion elementwise | flops 262144 | bytes 1572864 | tf_op jit(solution)/shard_map/convert_element_type | solution.py:33
  9.1 1.1 %multiply_convert_fusion = bf16[2,64,4096]{2,1,0:T(8,128)(2,1)} fusion(f32[2,4096]{1,0:T(2,128)S(1)} %convert_element_type.18, f32[64,4096]{1,0:T(8,128)S(1)} %convert_element_type.17), kind=kLoop, calls=%fused_computation.1 | loop fusion | flops 1048576 | bytes 2129920 | tf_op jit(solution)/shard_map/convert_element_type | solution.py:13
  10.3 24.0 %all-gather.4.cloned.1.call-done = bf16[256,4096]{1,0:T(8,128)(2,1)} async-done(((bf16[64,4096]{1,0:T(8,128)(2,1)}), bf16[256,4096]{1,0:T(8,128)(2,1)}) %all-gather.4.cloned.1.call-update) | async-done | bytes 2097168 | tf_op jit(solution)/shard_map/all_gather | solution.py:21
  34.2 0.0 copy-start
  34.2 2.9 %fusion.2 = f32[128,256]{1,0:T(8,128)S(1)} fusion(bf16[128,4096]{1,0:T(8,128)(2,1)} %bitcast.8, bf16[256,4096]{1,0:T(8,128)(2,1)} %all-gather.4.cloned.1.call-done), kind=kOutput, calls=%fused_computation.5 | convolution fusion | flops 268435456 | bytes 3276800 | tf_op jit(solution)/shard_map/rv,dv->rd/dot_general | solution.py:18
  37.1 38.3 %all-reduce.1 = bf16[128,256]{1,0:T(8,128)(2,1)S(1)} all-reduce(f32[128,256]{1,0:T(8,128)S(1)} %fusion.2), channel_id=1, replica_groups=mesh['blk'=4,'vox'=8] {'vox'}, use_global_device_ids=true, to_apply=%region_0.0 | all-reduce | flops 32768 | bytes 196608 | tf_op jit(solution)/shard_map/psum | solution.py:25
  75.5 0.0 copy-done
  75.5 0.5 multiply_reduce_fusion
  76.0 5.4 %all-gather.1 = f32[4,2,4096]{2,1,0:T(2,128)S(1)} all-gather(f32[1,2,4096]{2,1,0:T(2,128)S(1)} %bitcast.9), channel_id=2, replica_groups=mesh['blk'=4,'vox'=8] {'blk'}, dimensions={0}, use_global_device_ids=true | all-gather | bytes 163840 | tf_op jit(solution)/shard_map/all_gather | solution.py:34
  81.4 0.1 reduce_sum.19
  81.4 0.6 broadcast_multiply_fusion
Async XLA Ops:
  6.5 27.7 %all-gather.4.cloned.1.call-start = ((), (), s32[]{:S(2)}) async-start(), calls=%async_computation | async-start | bytes 2621440 | tf_op jit(solution)/shard_map/all_gather | solution.py:21
  34.2 41.2 %copy-start = (bf16[256,4096]{1,0:T(8,128)(2,1)S(1)}, bf16[256,4096]{1,0:T(8,128)(2,1)}, u32[]{:S(2)}) copy-start(bf16[256,4096]{1,0:T(8,128)(2,1)} %all-gather.4.cloned.1.call-done) | copy-start | bytes 6291460
Sparse Core Ops, SparseCore 0:
  8.9 25.2 all-gather.3
